TPU v7x, 32 devices: a whole 2x2x4 slice. The times are simulated.
32 devices in a mesh: rows: 8 (over z, y), cols: 4 (over x, core).
Axes of the slice: x: 2, y: 2, z: 4, core: 2. Of those that a mesh axis runs over, the one named last changes fastest.
Arguments:
- points: bfloat16 [4096, 256], P(('rows', 'cols')), may hold values from -6 to 6
- start_vectors: float32 [8, 4096], P(None, ('rows', 'cols')), may hold values from -6 to 6
- degree: bfloat16 [4096], P(('rows', 'cols')), may hold values from 0.19921875 to 2
Outputs:
- embedding: float32 [8, 4096], P(None, ('rows', 'cols'))
All inputs are finite; a program needn't handle non-finite values.
Results may differ from a plain program's by a relative error of at most 0.0034.
Values may be sent and summed in bfloat16 or wider, within the bound.
A program may use at most 64 MiB of HBM per device.

v0:
```python
import jax
import jax.numpy as jnp
from jax import lax
from jax.sharding import PartitionSpec as P

ITERS = 3


def body(points, start_vectors, degree):
    row_count = lax.axis_size("rows")
    col_count = lax.axis_size("cols")
    row_place = lax.axis_index("rows")
    col_place = lax.axis_index("cols")
    span_size = points.shape[0]
    sharpness = 4.0 / points.shape[1]
    row_points, row_degree = (
        lax.all_gather(points, "cols", axis=0, tiled=True),
        lax.all_gather(degree, "cols", axis=0, tiled=True),
    )
    row_total = row_points.shape[0]
    row_float = row_points.astype(jnp.float32)
    row_norms = jnp.sum(row_float * row_float, axis=1)
    row_slots = jnp.arange(row_total, dtype=jnp.int32)
    row_global = (
        row_place * col_count + row_slots // span_size
    ) * span_size + row_slots % span_size

    def kernel_block(x_block, col_norms, first_slot):
        inner = lax.dot_general(
            row_points, x_block, (((1,), (1,)), ((), ())), preferred_element_type=jnp.float32
        )
        distance = row_norms[:, None] + col_norms[None, :] - 2.0 * inner
        kernel = jnp.exp(-sharpness * distance)
        col_slots = first_slot + jnp.arange(x_block.shape[0], dtype=jnp.int32)
        col_global = (
            col_slots // span_size * col_count + col_place
        ) * span_size + col_slots % span_size
        return jnp.where(
            row_global[:, None] == col_global[None, :], jnp.float32(0.0), kernel
        ).astype(jnp.bfloat16)

    vectors = start_vectors
    for iteration in range(ITERS):
        empty = jnp.zeros((vectors.shape[0], row_total), jnp.float32)
        sending = vectors.T.astype(jnp.bfloat16)
        x_piece = lax.all_gather(points, "rows", axis=0, tiled=True)
        v_piece = lax.all_gather(sending, "rows", axis=0, tiled=True)
        piece_rows = x_piece.shape[0]
        block_size = 512
        block_count = piece_rows // block_size

        def accumulate(block_index, running):
            offset = block_index * block_size
            x_block = lax.dynamic_slice_in_dim(x_piece, offset, block_size, 0)
            v_block = lax.dynamic_slice_in_dim(v_piece, offset, block_size, 0)
            x_float = x_block.astype(jnp.float32)
            col_norms = jnp.sum(x_float * x_float, axis=1)
            kernel = kernel_block(x_block, col_norms, offset)
            return running + lax.dot_general(
                v_block, kernel, (((0,), (1,)), ((), ())), preferred_element_type=jnp.float32
            )

        partial_value = lax.fori_loop(0, block_count, accumulate, empty)
        summed = lax.psum(partial_value, "cols")
        row_state = summed / row_degree.astype(jnp.float32)[None, :]
        vectors = lax.dynamic_slice_in_dim(row_state, col_place * span_size, span_size, 1)
    magnitude = lax.psum(jnp.sum(jnp.abs(row_state), axis=1), "rows")
    mean_abs = magnitude / (span_size * row_count * col_count)
    return vectors / (mean_abs[:, None] + 1e-06)


def solution(mesh):
    return jax.shard_map(
        body,
        mesh=mesh,
        in_specs=(P(("rows", "cols"), None), P(None, ("rows", "cols")), P(("rows", "cols"))),
        out_specs=P(None, ("rows", "cols")),
        check_vma=False,
    )
```

profile of v0, /device:TPU:0, one launch (start us, length us, event | category | flops | bytes accessed | tf_op | source)
XLA Modules:
  0.0 177.6 jit_solution(2372064318550203494)
XLA Ops:
  0.0 0.7 copy-done.2
  0.7 6.0 %all-gather = bf16[4,1,128]{2,1,0:T(2,128)(2,1)S(1)} all-gather(bf16[1,1,128]{2,1,0:T(2,128)(2,1)S(1)} %bitcast.73), channel_id=1, replica_groups=mesh['rows'=8,'cols'=4] {'cols'}, dimensions={0}, use_global_device_ids=true | all-gather | bytes 1280 | tf_op jit(solution)/shard_map/all_gather | solution.py:18
  6.7 6.5 %all_gather.21 = bf16[512,256]{1,0:T(8,128)(2,1)S(1)} all-gather(bf16[128,256]{1,0:T(8,128)(2,1)} %param.9), channel_id=1, replica_groups=mesh['rows'=8,'cols'=4] {'cols'}, dimensions={0}, use_global_device_ids=true | all-gather | bytes 327680 | tf_op jit(solution)/shard_map/all_gather | solution.py:17
  13.4 0.7 copy-done
  14.0 32.1 %all_gather.22 = bf16[1024,256]{1,0:T(8,128)(2,1)S(1)} all-gather(bf16[128,256]{1,0:T(8,128)(2,1)S(1)} %copy-done), channel_id=1, replica_groups=mesh['rows'=8,'cols'=4] {'rows'}, dimensions={0}, use_global_device_ids=true | all-gather | bytes 589824 | tf_op jit(solution)/shard_map/all_gather | solution.py:46
  46.2 26.1 %all_gather.20 = bf16[1024,8]{0,1:T(8,128)(2,1)S(1)} all-gather(bf16[128,8]{0,1:T(8,128)(2,1)S(1)} %convert_bitcast_fusion), channel_id=1, replica_groups=mesh['rows'=8,'cols'=4] {'rows'}, dimensions={0}, use_global_device_ids=true | all-gather | bytes 18432 | tf_op jit(solution)/shard_map/all_gather | solution.py:47
  72.3 1.6 while.48
  72.5 0.6 fusion.155
  73.1 0.2 multiply_reduce_fusion.7
  73.3 0.6 fusion.155
  73.9 10.1 %psum.28 = f32[8,512]{1,0:T(8,128)S(1)} all-reduce(f32[8,512]{1,0:T(8,128)S(1)} %get-tuple-element.608), channel_id=1, replica_groups=mesh['rows'=8,'cols'=4] {'cols'}, use_global_device_ids=true, to_apply=%region_4.5 | all-reduce | flops 4096 | bytes 32768 | tf_op jit(solution)/shard_map/psum | solution.py:64
  84.0 26.1 %all_gather.24 = bf16[1024,8]{0,1:T(8,128)(2,1)S(1)} all-gather(bf16[128,8]{0,1:T(8,128)(2,1)S(1)} %fusion.131), channel_id=1, replica_groups=mesh['rows'=8,'cols'=4] {'rows'}, dimensions={0}, use_global_device_ids=true | all-gather | bytes 18432 | tf_op jit(solution)/shard_map/all_gather | solution.py:47
  110.1 1.6 while.49
  110.3 0.6 fusion.160
  110.9 0.2 multiply_reduce_fusion.8
  111.1 0.6 fusion.160
  111.7 10.1 %psum.29 = f32[8,512]{1,0:T(8,128)S(1)} all-reduce(f32[8,512]{1,0:T(8,128)S(1)} %get-tuple-element.609), channel_id=1, replica_groups=mesh['rows'=8,'cols'=4] {'cols'}, use_global_device_ids=true, to_apply=%region_8.9 | all-reduce | flops 4096 | bytes 32768 | tf_op jit(solution)/shard_map/psum | solution.py:64
  121.8 26.1 %all_gather.25 = bf16[1024,8]{0,1:T(8,128)(2,1)S(1)} all-gather(bf16[128,8]{0,1:T(8,128)(2,1)S(1)} %fusion.132), channel_id=1, replica_groups=mesh['rows'=8,'cols'=4] {'rows'}, dimensions={0}, use_global_device_ids=true | all-gather | bytes 18432 | tf_op jit(solution)/shard_map/all_gather | solution.py:47
  148.0 1.6 while.50
  148.1 0.6 fusion.165
  148.9 0.6 fusion.165
  149.5 10.1 %psum.30 = f32[8,512]{1,0:T(8,128)S(1)} all-reduce(f32[8,512]{1,0:T(8,128)S(1)} %get-tuple-element.610), channel_id=1, replica_groups=mesh['rows'=8,'cols'=4] {'cols'}, use_global_device_ids=true, to_apply=%region_12.13 | all-reduce | flops 4096 | bytes 32768 | tf_op jit(solution)/shard_map/psum | solution.py:64
  159.8 17.1 %psum.31 = f32[8]{0:T(128)S(1)} all-reduce(f32[8]{0:T(128)S(1)} %get-tuple-element.749), channel_id=1, replica_groups=mesh['rows'=8,'cols'=4] {'rows'}, use_global_device_ids=true, to_apply=%region_14.15 | all-reduce | flops 8 | bytes 64 | tf_op jit(solution)/shard_map/psum | solution.py:67
  176.9 0.7 dynamic-slice_divide_fusion.2
  (25 shorter events, 1.1 us)
Async XLA Ops:
  0.0 0.7 copy-start.2
  13.2 0.8 copy-start
  14.0 32.1 %copy-start.1 = (f32[8,128]{1,0:T(8,128)S(1)}, f32[8,128]{1,0:T(8,128)}, u32[]{:S(2)}) copy-start(f32[8,128]{1,0:T(8,128)} %param.10) | copy-start | bytes 12292
where the time goes:
time: 178 us
  blocking collectives  170 us (96%)
  matrix products  3.57 us (2%)
  other arithmetic  2.03 us (1%)
    all_gather x3, blocking collectives, body(): v_piece = lax.all_gather(sending, 'rows', axis=0, tiled=True)  78.3 us
    all_gather x1, blocking collectives, body(): x_piece = lax.all_gather(points, 'rows', axis=0, tiled=True)  32.1 us
    psum x3, blocking collectives, body(): summed = lax.psum(partial_value, 'cols')  30.4 us
    psum x1, blocking collectives, body(): magnitude = lax.psum(jnp.sum(jnp.abs(row_state), axis=1), 'rows')  17.1 us
    all_gather x1, blocking collectives, body(): lax.all_gather(points, 'cols', axis=0, tiled=True)  6.47 us
    all_gather x1, blocking collectives, body(): lax.all_gather(degree, 'cols', axis=0, tiled=True)  5.99 us
    dot_general x6, matrix products, accumulate(): lax.dot_general(v_block, kernel, (((0,), (1,)), ((), ())), preferred_elem...  3.57 us

commit v1 on v0

--- a/solution.py
+++ b/solution.py
@@ -61,7 +61,9 @@
             )
 
         partial_value = lax.fori_loop(0, block_count, accumulate, empty)
-        summed = lax.psum(partial_value, "cols")
+        summed = partial_value
+        for hop in (1, 2):
+            summed = summed + lax.ppermute(summed, "cols", [(dev, dev ^ hop) for dev in range(4)])
         row_state = summed / row_degree.astype(jnp.float32)[None, :]
         vectors = lax.dynamic_slice_in_dim(row_state, col_place * span_size, span_size, 1)
     magnitude = lax.psum(jnp.sum(jnp.abs(row_state), axis=1), "rows")

time: 178 us -> 160 us (0.90)
  blocking collectives: 170 us -> 140 us
  waiting for transfers between devices: 0 us -> 10 us
  starting transfers between devices: 0 us -> 2.56 us
    psum x3 -> x0, blocking collectives: 30.4 us -> none  [body(): summed = lax.psum(partial_value, 'cols')]
    ppermute x0 -> x6, waiting for transfers between devices: none -> 10 us  [body(): lax.ppermute(summed, 'cols', [(dev, dev ^ hop) for dev in range(4)])]
    ppermute x0 -> x6, starting transfers between devices: none -> 2.56 us  [body(): lax.ppermute(summed, 'cols', [(dev, dev ^ hop) for dev in range(4)])]
  transfers between devices with their start and end apart: 0 -> 6, of which waited for: 0 -> 5; matrix products, arithmetic and copies ran while one was open for 0% -> 0% of each run, Pallas kernels for 0% -> 0%
where the time goes in v1:
time: 160 us
  blocking collectives  140 us (88%)
  waiting for transfers between devices  10 us (6%)
  matrix products  3.57 us (2%)
  starting transfers between devices  2.56 us (2%)
  other arithmetic  2.04 us (1%)
    all_gather x3, blocking collectives, body(): v_piece = lax.all_gather(sending, 'rows', axis=0, tiled=True)  78.3 us
    all_gather x1, blocking collectives, body(): x_piece = lax.all_gather(points, 'rows', axis=0, tiled=True)  31.9 us
    psum x1, blocking collectives, body(): magnitude = lax.psum(jnp.sum(jnp.abs(row_state), axis=1), 'rows')  17.1 us
    ppermute x6, waiting for transfers between devices, body(): lax.ppermute(summed, 'cols', [(dev, dev ^ hop) for dev in range(4)])  10 us
    all_gather x1, blocking collectives, body(): lax.all_gather(points, 'cols', axis=0, tiled=True)  7.55 us
    all_gather x1, blocking collectives, body(): lax.all_gather(degree, 'cols', axis=0, tiled=True)  5.05 us
    dot_general x6, matrix products, accumulate(): lax.dot_general(v_block, kernel, (((0,), (1,)), ((), ())), preferred_elem...  3.57 us
  transfers between devices with their start and end apart: 6, of which 5 were waited for; matrix products, arithmetic and copies ran while one was open for 0% of the time, Pallas kernels for 0%

profile of v1, /device:TPU:0, one launch (start us, length us, event | category | flops | bytes accessed | tf_op | source)
XLA Modules:
  0.0 159.7 jit_solution(17150227175480588680)
XLA Ops:
  0.0 7.5 %all_gather.21 = bf16[512,256]{1,0:T(8,128)(2,1)S(1)} all-gather(bf16[128,256]{1,0:T(8,128)(2,1)} %param.9), channel_id=1, replica_groups=mesh['rows'=8,'cols'=4] {'cols'}, dimensions={0}, use_global_device_ids=true | all-gather | bytes 327680 | tf_op jit(solution)/shard_map/all_gather | solution.py:17
  7.6 31.9 %all_gather.22 = bf16[1024,256]{1,0:T(8,128)(2,1)S(1)} all-gather(bf16[128,256]{1,0:T(8,128)(2,1)S(1)} %copy-done), channel_id=1, replica_groups=mesh['rows'=8,'cols'=4] {'rows'}, dimensions={0}, use_global_device_ids=true | all-gather | bytes 589824 | tf_op jit(solution)/shard_map/all_gather | solution.py:46
  39.7 0.7 copy-done.1
  40.3 26.1 %all_gather.20 = bf16[1024,8]{0,1:T(8,128)(2,1)S(1)} all-gather(bf16[128,8]{0,1:T(8,128)(2,1)S(1)} %convert_bitcast_fusion), channel_id=1, replica_groups=mesh['rows'=8,'cols'=4] {'rows'}, dimensions={0}, use_global_device_ids=true | all-gather | bytes 18432 | tf_op jit(solution)/shard_map/all_gather | solution.py:47
  66.4 1.6 while.48
  66.6 0.6 fusion.157
  68.0 1.2 collective-permute-done
  69.2 1.5 collective-permute-start.1
  70.7 0.7 copy-done.2
  71.4 5.0 %all-gather = bf16[4,1,128]{2,1,0:T(2,128)(2,1)S(1)} all-gather(bf16[1,1,128]{2,1,0:T(2,128)(2,1)S(1)} %bitcast.73), channel_id=1, replica_groups=mesh['rows'=8,'cols'=4] {'cols'}, dimensions={0}, use_global_device_ids=true | all-gather | bytes 1280 | tf_op jit(solution)/shard_map/all_gather | solution.py:18
  76.5 26.1 %all_gather.24 = bf16[1024,8]{0,1:T(8,128)(2,1)S(1)} all-gather(bf16[128,8]{0,1:T(8,128)(2,1)S(1)} %fusion.133), channel_id=1, replica_groups=mesh['rows'=8,'cols'=4] {'rows'}, dimensions={0}, use_global_device_ids=true | all-gather | bytes 18432 | tf_op jit(solution)/shard_map/all_gather | solution.py:47
  102.6 1.6 while.49
  102.8 0.6 fusion.162
  103.6 0.6 fusion.162
  104.2 1.2 collective-permute-done.2
  106.0 3.2 %collective-permute-done.3 = f32[8,512]{1,0:T(8,128)S(1)} collective-permute-done((f32[8,512]{1,0:T(8,128)S(1)}, f32[8,512]{1,0:T(8,128)S(1)}, u32[]{:S(2)}, u32[]{:S(2)}) %collective-permute-start.3) | collective-permute-done | bytes 16416 | tf_op jit(solution)/shard_map/ppermute | solution.py:66
  109.2 26.1 %all_gather.25 = bf16[1024,8]{0,1:T(8,128)(2,1)S(1)} all-gather(bf16[128,8]{0,1:T(8,128)(2,1)S(1)} %fusion.134), channel_id=1, replica_groups=mesh['rows'=8,'cols'=4] {'rows'}, dimensions={0}, use_global_device_ids=true | all-gather | bytes 18432 | tf_op jit(solution)/shard_map/all_gather | solution.py:47
  135.3 1.6 while.50
  135.5 0.6 fusion.167
  136.3 0.6 fusion.167
  136.8 1.2 collective-permute-done.4
  138.6 3.2 %collective-permute-done.5 = f32[8,512]{1,0:T(8,128)S(1)} collective-permute-done((f32[8,512]{1,0:T(8,128)S(1)}, f32[8,512]{1,0:T(8,128)S(1)}, u32[]{:S(2)}, u32[]{:S(2)}) %collective-permute-start.5) | collective-permute-done | bytes 16416 | tf_op jit(solution)/shard_map/ppermute | solution.py:66
  141.9 17.1 %psum.7 = f32[8]{0:T(128)S(1)} all-reduce(f32[8]{0:T(128)S(1)} %get-tuple-element.749), channel_id=1, replica_groups=mesh['rows'=8,'cols'=4] {'rows'}, use_global_device_ids=true, to_apply=%region_11.12 | all-reduce | flops 8 | bytes 64 | tf_op jit(solution)/shard_map/psum | solution.py:69
  159.1 0.7 dynamic-slice_divide_fusion
  (37 shorter events, 3.1 us)
Async XLA Ops:
  0.0 7.6 %copy-start = (bf16[128,256]{1,0:T(8,128)(2,1)S(1)}, bf16[128,256]{1,0:T(8,128)(2,1)}, u32[]{:S(2)}) copy-start(bf16[128,256]{1,0:T(8,128)(2,1)} %param.9) | copy-start | bytes 196612
  39.6 0.7 copy-start.1
  68.0 1.2 collective-permute-start
  69.2 7.3 %collective-permute-start.1 = (f32[8,512]{1,0:T(8,128)S(1)}, f32[8,512]{1,0:T(8,128)S(1)}, u32[]{:S(2)}, u32[]{:S(2)}) collective-permute-start(f32[8,512]{1,0:T(8,128)S(1)} %add.529), channel_id=1, source_target_pairs={{0,2},{1,3},{2,0},{3,1},{4,6},{5,7},{6,4},{7,5},{8,10},{9,11},{10,... | collective-permute-start | bytes 49160 | tf_op jit(solution)/shard_map/ppermute | solution.py:66
  70.7 0.7 copy-start.2
  104.2 1.2 collective-permute-start.2
  105.4 3.7 %collective-permute-start.3 = (f32[8,512]{1,0:T(8,128)S(1)}, f32[8,512]{1,0:T(8,128)S(1)}, u32[]{:S(2)}, u32[]{:S(2)}) collective-permute-start(f32[8,512]{1,0:T(8,128)S(1)} %add.532), channel_id=1, source_target_pairs={{0,2},{1,3},{2,0},{3,1},{4,6},{5,7},{6,4},{7,5},{8,10},{9,11},{10,... | collective-permute-start | bytes 49160 | tf_op jit(solution)/shard_map/ppermute | solution.py:66
  136.8 1.2 collective-permute-start.4
  138.1 3.7 %collective-permute-start.5 = (f32[8,512]{1,0:T(8,128)S(1)}, f32[8,512]{1,0:T(8,128)S(1)}, u32[]{:S(2)}, u32[]{:S(2)}) collective-permute-start(f32[8,512]{1,0:T(8,128)S(1)} %add.534), channel_id=1, source_target_pairs={{0,2},{1,3},{2,0},{3,1},{4,6},{5,7},{6,4},{7,5},{8,10},{9,11},{10,... | collective-permute-start | bytes 49160 | tf_op jit(solution)/shard_map/ppermute | solution.py:66
